TPU v7x, 512 devices: a whole 4x8x8 slice. The times are simulated.
512 devices in a mesh: dp: 8 (over z), vocab: 64 (over x, y, core).
Axes of the slice: x: 4, y: 8, z: 8, core: 2. Of those that a mesh axis runs over, the one named last changes fastest.
Arguments:
- hidden: bfloat16 [384, 8192], P('dp', 'vocab'), may hold values from -90 to 90
- weight: bfloat16 [8192, 152064], P('dp', 'vocab'), may hold values from -0.1875 to 0.1875
- targets: int32 [384], P('dp'), may hold values from 0 to 152063
- pad_mask: int32 [384], P('dp'), may hold values from 0 to 1
Outputs:
- token_nll: float32 [384], P('dp')
- nll_total: float32 [], replicated
All inputs are finite; a program needn't handle non-finite values.
Results may differ from a plain program's by a relative error of at most 0.0003.
Values may be sent and summed in bfloat16 or wider, within the bound.
A program may use at most 64 MiB of HBM per device.

v0:
```python
import jax
import jax.numpy as jnp
from jax import lax
from jax.sharding import PartitionSpec as P


def from_everyone(shard, axis):
    copies = jnp.broadcast_to(shard, (lax.axis_size(axis), *shard.shape))
    return lax.all_to_all(copies, axis, split_axis=0, concat_axis=0, tiled=True)


def joined_along(tiles, dim):
    shape = list(tiles.shape[1:])
    shape[dim] *= tiles.shape[0]
    return jnp.moveaxis(tiles, 0, dim).reshape(shape)


def gather_directly(shard, axis, dim):
    tiles = from_everyone(shard, axis)
    return joined_along(tiles, dim)


def gathered_once(shard, axis):
    leaves = jax.tree.leaves(shard)
    order = sorted(range(len(leaves)), key=lambda k: -leaves[k].size)
    width = (1, *leaves[order[0]].shape)[-1]
    lines = [
        jnp.pad(leaves[k].reshape(-1), (0, -leaves[k].size % width)).reshape(-1, width)
        for k in order
    ]
    both, at, found = (from_everyone(jnp.concatenate(lines), axis), 0, {})
    for k, line in zip(order, lines):
        share = both[:, at : at + len(line)].reshape(len(both), -1)
        found[k] = share[:, : leaves[k].size].reshape(-1, *leaves[k].shape)
        at += len(line)
    numbers = iter(range(len(leaves)))
    return jax.tree.map(lambda _: found[next(numbers)], shard)


def joined_by_halves(pieces, combine):
    while len(jax.tree.leaves(pieces)[0]) > 1:
        pieces = jax.vmap(combine)(
            *(jax.tree.map(lambda part: part[side::2], pieces) for side in (0, 1))
        )
    return jax.tree.map(lambda part: part[0], pieces)


def merged_2(shard, axis, combine):
    pieces = gathered_once(shard, axis)
    return joined_by_halves(pieces, combine)


def taken_together(shard, axis):
    everything = from_everyone(shard, axis)
    return jnp.sum(everything, axis=0)


def join_stats(earlier, later):
    max_one, sum_one, pick_one = earlier
    max_two, sum_two, pick_two = later
    merged = jnp.maximum(max_one, max_two)
    return (
        merged,
        sum_one * jnp.exp(max_one - merged) + sum_two * jnp.exp(max_two - merged),
        pick_one + pick_two,
    )


def per_device(hidden, weight, targets, pad_mask):
    whole_width = gather_directly(hidden, "vocab", 1)
    n_cols = weight.shape[1]
    spread = lax.all_to_all(whole_width, "dp", split_axis=1, concat_axis=0, tiled=True)
    logits = lax.psum_scatter(
        jnp.dot(spread, weight, preferred_element_type=jnp.float32),
        "dp",
        scatter_dimension=0,
        tiled=True,
    )
    col_base = lax.axis_index("vocab") * n_cols
    column_ids = lax.broadcasted_iota(jnp.int32, (1, n_cols), 1) + col_base
    is_target = column_ids == targets[:, None]
    local_pick = jnp.sum(jnp.where(is_target, logits, 0.0), axis=1)
    local_max = jnp.max(logits, axis=1)
    local_sum = jnp.sum(jnp.exp(logits - local_max[:, None]), axis=1)
    row_max, exp_sum, picked = merged_2((local_max, local_sum, local_pick), "vocab", join_stats)
    token_nll = pad_mask.astype(jnp.float32) * (row_max + jnp.log(exp_sum) - picked)
    nll_total = taken_together(jnp.sum(token_nll), "dp")
    return (token_nll, nll_total)


def solution(mesh):
    placed = (P("dp", "vocab"), P("dp", "vocab"), P("dp"), P("dp"))
    return jax.shard_map(
        per_device, mesh=mesh, in_specs=placed, out_specs=(P("dp"), P()), check_vma=False
    )
```

profile of v0, /device:TPU:1, one launch (start us, length us, event | category | flops | bytes accessed | tf_op | source)
XLA Modules:
  0.0 173.9 jit_solution(11742565139801301044)
XLA Ops:
  7.2 0.0 reduce-scatter.2.cloned.1.call-start
  7.2 0.8 broadcast_in_dim.15
  8.0 34.3 %all_to_all.35 = bf16[64,48,128]{2,1,0:T(8,128)(2,1)S(1)} all-to-all(bf16[64,48,128]{2,1,0:T(8,128)(2,1)S(1)} %broadcast_in_dim.15), channel_id=1, replica_groups=mesh['dp'=8,'vocab'=64] {'vocab'}, dimensions={0} | all-to-all | bytes 1572864 | tf_op jit(solution)/shard_map/all_to_all | solution.py:9
  42.4 0.2 copy.15
  42.6 0.3 all_to_all.25
  42.9 0.4 copy.16
  43.3 32.1 %all_to_all.36 = bf16[48,8,1024]{2,0,1:T(8,128)(2,1)S(1)} all-to-all(bf16[48,8,1024]{2,0,1:T(8,128)(2,1)S(1)} %copy.16), channel_id=1, replica_groups=mesh['dp'=8,'vocab'=64] {'dp'}, dimensions={1} | all-to-all | bytes 1572864 | tf_op jit(solution)/shard_map/all_to_all | solution.py:72
  75.4 0.0 copy-start.1
  75.4 6.4 %fusion.4 = f32[384,2376]{1,0:T(8,128)} fusion(bf16[384,1024]{1,0:T(8,128)(2,1)S(1)} %bitcast.20, bf16[1024,2376]{0,1:T(8,128)(2,1)} %param.5), kind=kOutput, calls=%fused_computation.15 | convolution fusion | flops 1868562432 | bytes 9302016 | tf_op jit(solution)/shard_map/dot_general | solution.py:74
  81.9 0.0 copy-start
  81.9 0.0 reduce-scatter.2.cloned.1.call-update
  81.9 47.3 %reduce-scatter.2.cloned.1.call-done = f32[48,2376]{1,0:T(8,128)} async-done(((f32[384,2376]{1,0:T(8,128)}), f32[48,2376]{1,0:T(8,128)}) %reduce-scatter.2.cloned.1.call-update) | async-done | bytes 456208 | tf_op jit(solution)/shard_map/reduce_scatter | solution.py:73
  129.2 1.1 reduce_max.9
  130.4 0.0 copy-done.1
  130.4 1.3 exponential_reduce_fusion
  131.8 0.2 reshape.45
  131.9 20.0 %all_to_all.37 = f32[64,1,144]{2,1,0:T(1,128)S(1)} all-to-all(f32[64,1,144]{2,1,0:T(1,128)S(1)} %reshape.45), channel_id=1, replica_groups=mesh['dp'=8,'vocab'=64] {'vocab'}, dimensions={0} | all-to-all | bytes 73728 | tf_op jit(solution)/shard_map/all_to_all | solution.py:9
  151.9 0.5 broadcast.8
  152.4 0.8 reduce.1
  153.2 0.1 reshape.46
  153.4 0.1 fusion.3
  154.1 0.0 copy-done
  154.1 1.1 fusion.2
  155.3 0.6 broadcast_in_dim.18
  155.9 10.5 %all_to_all.38 = f32[8,1,1]{2,1,0:T(1,128)S(1)} all-to-all(f32[8,1,1]{2,1,0:T(1,128)S(1)} %broadcast_in_dim.18), channel_id=1, replica_groups=mesh['dp'=8,'vocab'=64] {'dp'}, dimensions={0} | all-to-all | bytes 64 | tf_op jit(solution)/shard_map/all_to_all | solution.py:9
  166.4 0.6 reduce_sum.39
  (43 shorter events, 0.7 us)
Async XLA Ops:
  7.2 122.1 %reduce-scatter.2.cloned.1.call-start = ((), (), s32[]{:S(2)}) async-start(), calls=%async_computation.5 | async-start | bytes 4202496 | tf_op jit(solution)/shard_map/reduce_scatter | solution.py:73
  75.4 54.9 %copy-start.1 = (s32[48]{0:T(128)S(1)}, s32[48]{0:T(128)}, u32[]{:S(2)}) copy-start(s32[48]{0:T(128)} %param.6) | copy-start | bytes 580
  81.9 72.3 %copy-start = (s32[48]{0:T(128)S(1)}, s32[48]{0:T(128)}, u32[]{:S(2)}) copy-start(s32[48]{0:T(128)} %param.7) | copy-start | bytes 580
Sparse Core Ops, SparseCore 0:
  82.0 47.1 reduce-scatter.1
where the time goes:
time: 174 us
  blocking collectives  96.9 us (56%)
  waiting for transfers between devices  47.3 us (27%)
  between operations  14.2 us (8%)
  matrix products  6.42 us (4%)
  other arithmetic  5.12 us (3%)
  local copies, waits for them, and re-layouts  3.84 us (2%)
    all_to_all x3, blocking collectives, from_everyone(): return lax.all_to_all(copies, axis, split_axis=0, concat_axis=0, tiled=True)  64.9 us
    reduce_scatter x1, waiting for transfers between devices, per_device(): lax.psum_scatter(jnp.dot(spread, weight, preferred_element_type=jnp.float...  47.3 us
    all_to_all x1, blocking collectives, per_device(): lax.all_to_all(whole_width, 'dp', split_axis=1, concat_axis=0, tiled=True)  32.1 us
    dot_general x1, matrix products, per_device(): jnp.dot(spread, weight, preferred_element_type=jnp.float32)  6.42 us
  transfers between devices with their start and end apart: 1, of which 1 were waited for; matrix products, arithmetic and copies ran while one was open for 0% of the time, Pallas kernels for 0%

commit v1 on v0

v1 whole, which is shorter than its diff:
```python
import functools

import jax
import jax.numpy as jnp
from jax import lax
from jax.experimental import pallas as pl
from jax.experimental.pallas import tpu as pltpu
from jax.sharding import PartitionSpec as P

NZ, NX, NY, NC = 8, 4, 8, 2
T = 48
D = 128
CH = 16
NCH = T // CH
LN2 = 0.6931471805599453
TOP = 32766.0
F32 = jnp.float32


def kernel(V, VP, hid, weight, tgt, msk, nll_out, tot_out,
           H, W, ACC, SB, RB, TQ, MQ, MB1, MB2, MB3,
           w_sem, zs_sem, own_r, s1_s, s2_s, s3_s, s3_r, s4_s, s4_r,
           q_s, q_r, ring_s, ring_r, m_s, m_r):
    z = lax.axis_index("dp")
    v = lax.axis_index("vocab")
    c = lax.rem(v, NC)
    y = lax.rem(lax.div(v, NC), NY)
    x = lax.div(v, NC * NY)
    r = lax.rem(y, 4)
    xc = x * NC + c
    sg = 1 - 2 * c

    def at(zz=z, xx=x, yy=y, cc=c):
        return (zz, (xx * NY + yy) * NC + cc)

    def remote(src, dst, ss, rs, dev):
        return pltpu.make_async_remote_copy(
            src_ref=src, dst_ref=dst, send_sem=ss, recv_sem=rs,
            device_id=dev, device_id_type=pl.DeviceIdType.MESH)

    wcopies = []
    for cc in range(NC):
        for rr in range(4):
            wcopies.append(pltpu.make_async_copy(
                weight.at[pl.ds((rr * NC + cc) * D, D)],
                W.at[pl.ds((cc * 4 + rr) * D, D)], w_sem.at[cc * 4 + rr]))
    for cp in wcopies:
        cp.start()

    def xc_peer(d):
        o = lax.rem(xc + d, 8)
        return o, at(xx=lax.div(o, NC), cc=lax.rem(o, NC))

    def y_peer(d):
        o = lax.rem(y + d, NY)
        return o, at(yy=o)

    def z_peer(d):
        o = lax.rem(z + d, NZ)
        return o, at(zz=o)

    peers = (xc_peer, y_peer, z_peer)
    barrier = pltpu.get_barrier_semaphore()
    for peer in peers:
        for d in range(1, 8):
            pl.semaphore_signal(barrier, inc=1, device_id=peer(d)[1],
                                device_id_type=pl.DeviceIdType.MESH)
    pl.semaphore_wait(barrier, 21)

    def rows(o):
        return pl.ds(pl.multiple_of(o * T, CH), T)

    kd = 2 * x + lax.div(y, 4)
    zoff = lax.rem(z - kd + NZ, NZ)
    zmove = remote(hid, H.at[c, r, rows(zoff)], zs_sem, own_r.at[zoff], at(zz=kd))
    zlocal = pltpu.make_async_copy(hid, H.at[c, r, rows(zoff)], own_r.at[zoff])

    @pl.when(z != kd)
    def _():
        zmove.start()

    @pl.when(z == kd)
    def _():
        zlocal.start()

    opp = lax.rem(z + 4, NZ)
    tcopy = remote(tgt, TQ, q_s.at[0], q_r.at[0], at(zz=opp))
    mcopy = remote(msk, MQ, q_s.at[1], q_r.at[1], at(zz=opp))
    tcopy.start()
    mcopy.start()

    xs = lax.div(z, 2)
    in_col = x == xs
    is_src = jnp.logical_and(in_col, lax.div(y, 4) == lax.rem(z, 2))

    def s1(o):
        b = H.at[c, r, rows(o)]
        return remote(b, b, s1_s.at[o], own_r.at[o], at(yy=lax.rem(y + 4, NY)))

    def s2(o, d):
        b = H.at[c, r, rows(o)]
        return remote(b, b, s2_s.at[o, d - 1], own_r.at[o], at(xx=lax.rem(x + d, NX)))

    steps3 = (1, NY - 1, 2 * sg + NY)

    def s3(o, n):
        b = H.at[c, r, rows(o)]
        return remote(b, b, s3_s.at[o, n], s3_r.at[o, n], at(yy=lax.rem(y + steps3[n], NY)))

    def s4(o):
        b = H.at[c, :, rows(o)]
        return remote(b, b, s4_s.at[o], s4_r.at[o], at(cc=1 - c))

    def take_own(o):
        zlocal_o = pltpu.make_async_copy(hid, H.at[c, r, rows(o)], own_r.at[o])
        zlocal_o.wait()

        @pl.when(is_src)
        def _():
            s1(o).start()

        @pl.when(in_col)
        def _():
            for d in range(1, NX):
                s2(o, d).start()

        for n in range(3):
            s3(o, n).start()

    def take_y(o):
        for n in range(3):
            s3(o, n).wait_recv()
        s4(o).start()

    def take_core(o):
        s4(o).wait_recv()

    lane = lax.broadcasted_iota(jnp.int32, (CH, VP), 1)
    valid = lane < V

    def mm(n, o):
        o = lax.rem(o + NZ, NZ)
        rs = rows(o)
        lhs = jnp.concatenate([H[cc, rr, rs, :] for cc in range(NC) for rr in range(4)], axis=1)
        main = V // 256 * 256
        for a in range(0, main, 768):
            w = min(768, main - a)
            ACC[n, :, a:a + w] = jnp.dot(lhs, W[:, a:a + w], preferred_element_type=F32)
        if main < V:
            ACC[n, :, main:V] = jnp.dot(lhs, W[:, main:V], preferred_element_type=F32)

    def taken(n, k):
        q = RB[n, pl.ds(k * CH, CH), :].astype(F32)
        g = jnp.exp(q[:, VP - 1:VP] * (LN2 / 64)) * (1.0 / TOP)
        return q * g

    def ring(n, k, dz):
        b = pl.ds(k * CH, CH)
        return remote(SB.at[n, b], RB.at[n, b], ring_s.at[n, k], ring_r.at[n, k],
                      at(zz=lax.rem(z + dz + NZ, NZ)))

    def send(n, k, val, dz):
        top = jnp.max(jnp.where(valid, jnp.abs(val), 0.0), axis=1, keepdims=True)
        code = jnp.ceil(jnp.log(jnp.maximum(top, 1e-30)) * (64 / LN2)) + 1.0
        q = val * (jnp.exp(code * (-LN2 / 64)) * TOP)
        SB[n, pl.ds(k * CH, CH), :] = jnp.round(jnp.where(valid, q, code)).astype(jnp.int16)
        ring(n, k, dz).start()

    def first(n, dz):
        for k in range(NCH):
            send(n, k, ACC[n, pl.ds(k * CH, CH), :], dz)

    def onward(n, k, dz):
        ring(n - 1, k, dz).wait_recv()
        send(n, k, ACC[n, pl.ds(k * CH, CH), :] + taken(n - 1, k), dz)

    take_own(0)
    take_own(1)
    take_own(7)
    take_y(0)
    take_own(2)
    take_own(6)
    take_core(0)
    for cp in wcopies:
        cp.wait()
    mm(0, 0)
    first(0, sg)
    take_y(1)
    take_y(7)
    take_own(3)
    take_own(5)
    take_own(4)
    take_core(1)
    take_core(7)
    mm(4, sg)
    first(4, -sg)
    mm(1, -sg)
    take_y(2)
    take_y(6)
    take_y(3)
    take_y(5)
    take_y(4)
    take_core(2)
    take_core(6)
    mm(5, 2 * sg)
    for k in range(NCH):
        onward(1, k, sg)
        onward(5, k, -sg)
    take_core(3)
    take_core(5)
    take_core(4)
    mm(2, -2 * sg)
    mm(6, 3 * sg)
    for k in range(NCH):
        onward(2, k, sg)
        onward(6, k, -sg)
    mm(3, -3 * sg)
    mm(7, 4 * sg)
    for k in range(NCH):
        onward(3, k, sg)

    tcopy.wait_recv()
    mcopy.wait_recv()
    ri = lax.broadcasted_iota(jnp.int32, (T, T), 0)
    ci = lax.broadcasted_iota(jnp.int32, (T, T), 1)
    tcol = jnp.sum(jnp.where(ri == ci, TQ[...].astype(F32), 0.0), axis=1, keepdims=True).astype(jnp.int32)
    ids = jnp.where(valid, lane + v * V, -1)
    cols = []
    for k in range(NCH):
        b = pl.ds(k * CH, CH)
        ring(3, k, sg).wait_recv()
        ring(6, k, -sg).wait_recv()
        val = ACC[7, b, :] + taken(3, k) + taken(6, k)
        val = jnp.where(valid, val, -3e38)
        top = jnp.max(val, axis=1, keepdims=True)
        s = jnp.sum(jnp.exp(val - top), axis=1, keepdims=True)
        p = jnp.sum(jnp.where(ids == tcol[k * CH:(k + 1) * CH], val, 0.0), axis=1, keepdims=True)
        cols.append((top, s, p))

    rl = lax.broadcasted_iota(jnp.int32, (T, 128), 0)
    ll = lax.broadcasted_iota(jnp.int32, (T, 128), 1)

    def as_row(n):
        col = jnp.concatenate([t[n] for t in cols], axis=0)
        return jnp.sum(jnp.where(rl == ll, col, 0.0), axis=0, keepdims=True)

    def exchange(MB, me, peer, base, rws):
        for n, row in enumerate(rws):
            MB[me, n:n + 1, :] = row
        cps = []
        for d in range(1, 8):
            o, dev = peer(d)
            cps.append(remote(MB.at[me], MB.at[me], m_s.at[base, d], m_r.at[base, me], dev))
        for cp in cps:
            cp.start()
        for d in range(1, 8):
            o, dev = peer(d)
            remote(MB.at[o], MB.at[o], m_s.at[base, d], m_r.at[base, o], dev).wait_recv()
        return cps

    def merged(MB):
        ms = [MB[j, 0:1, :] for j in range(8)]
        top = functools.reduce(jnp.maximum, ms)
        s = sum(MB[j, 1:2, :] * jnp.exp(ms[j] - top) for j in range(8))
        p = sum(MB[j, 2:3, :] for j in range(8))
        return top, s, p

    left = exchange(MB1, xc, xc_peer, 0, (as_row(0), as_row(1), as_row(2)))
    left += exchange(MB2, y, y_peer, 1, merged(MB1))
    top, s, p = merged(MB2)
    inside = lax.broadcasted_iota(jnp.int32, (1, 128), 1) < T
    nll = jnp.where(inside, top + jnp.log(jnp.where(inside, s, 1.0)) - p, 0.0)[:, :T]
    nll = MQ[...].astype(F32) * nll
    total = jnp.sum(nll, axis=1, keepdims=True)
    nll128 = jnp.concatenate([nll, jnp.zeros((1, 128 - T), F32)], axis=1)
    left += exchange(MB3, z, z_peer, 2, (nll128, jnp.broadcast_to(total, (1, 128))))
    nll_out[...] = MB3[opp, 0:1, :][:, :T]
    tot_out[...] = sum(MB3[j, 1:2, :] for j in range(8))[:, 0:1]

    @pl.when(z != kd)
    def _():
        zmove.wait_send()

    tcopy.wait_send()
    mcopy.wait_send()
    for o in range(NZ):
        @pl.when(is_src)
        def _():
            s1(o).wait_send()

        @pl.when(in_col)
        def _():
            for d in range(1, NX):
                s2(o, d).wait_send()

        for n in range(3):
            s3(o, n).wait_send()
        s4(o).wait_send()
    for n in range(7):
        for k in range(NCH):
            ring(n, k, sg).wait_send()
    for cp in left:
        cp.wait_send()


def per_device(hidden, weight, targets, pad_mask):
    V = weight.shape[1]
    VP = -(-(V + 1) // 128) * 128
    K = weight.shape[0]
    vmem = pl.BlockSpec(memory_space=pltpu.VMEM)
    dma = pltpu.SemaphoreType.DMA
    nll, tot = pl.pallas_call(
        functools.partial(kernel, V, VP),
        out_shape=(jax.ShapeDtypeStruct((1, T), F32), jax.ShapeDtypeStruct((1, 1), F32)),
        in_specs=[vmem, pl.BlockSpec(memory_space=pl.ANY), vmem, vmem],
        out_specs=(vmem, vmem),
        scratch_shapes=[
            pltpu.VMEM((NC, 4, NZ * T, D), jnp.bfloat16),
            pltpu.VMEM((K, V), jnp.bfloat16),
            pltpu.VMEM((8, T, VP), F32),
            pltpu.VMEM((7, T, VP), jnp.int16),
            pltpu.VMEM((7, T, VP), jnp.int16),
            pltpu.VMEM((1, T), jnp.int32),
            pltpu.VMEM((1, T), jnp.int32),
            pltpu.VMEM((8, 8, 128), F32),
            pltpu.VMEM((8, 8, 128), F32),
            pltpu.VMEM((8, 8, 128), F32),
            dma((8,)), dma, dma((8,)), dma((8,)), dma((8, 3)), dma((8, 3)), dma((8, 3)),
            dma((8,)), dma((8,)), dma((2,)), dma((2,)), dma((7, NCH)), dma((7, NCH)),
            dma((3, 8)), dma((3, 8)),
        ],
        compiler_params=pltpu.CompilerParams(collective_id=0, has_side_effects=True),
    )(hidden, weight, targets.reshape(1, T), pad_mask.reshape(1, T))
    return nll.reshape(T), tot.reshape(())


def solution(mesh):
    placed = (P("dp", "vocab"), P("dp", "vocab"), P("dp"), P("dp"))
    return jax.shard_map(
        per_device, mesh=mesh, in_specs=placed, out_specs=(P("dp"), P()), check_vma=False
    )
```

time: 174 us -> 82.3 us (0.47)
  blocking collectives: 96.9 us -> 0 us
  Pallas kernels: 0 us -> 70.3 us
  waiting for transfers between devices: 47.3 us -> 0 us
  between operations: 14.2 us -> 2.33 us
  matrix products: 6.42 us -> 0 us
  other arithmetic: 5.12 us -> 0 us
  local copies, waits for them, and re-layouts: 3.84 us -> 8.6 us
    all_to_all x4 -> x0, blocking collectives: 96.9 us -> none  [the longest x3 64.9 us: from_everyone(): return lax.all_to_all(copies, axis, split_axis=0, concat_axis=0, tiled=True)]
    pallas_call x0 -> x1, Pallas kernels: none -> 70.3 us  [per_device(): pl.pallas_call(functools.partial(kernel, V, VP), out_shape=(jax.ShapeDtyp...]
    reduce_scatter x1 -> x0, waiting for transfers between devices: 47.3 us -> none  [per_device(): lax.psum_scatter(jnp.dot(spread, weight, preferred_element_type=jnp.float...]
    unnamed x6 -> x2, local copies, waits for them, and re-layouts: 0.27 us -> 8.6 us
    dot_general x1 -> x0, matrix products: 6.42 us -> none  [per_device(): jnp.dot(spread, weight, preferred_element_type=jnp.float32)]
    reduce_sum x3 -> x0, other arithmetic: 3.06 us -> none  [the longest x1 1.31 us: per_device(): local_sum = jnp.sum(jnp.exp(logits - local_max[:, None]), axis=1)]
  transfers between devices with their start and end apart: 1 -> 0, of which waited for: 1 -> 0; matrix products, arithmetic and copies ran while one was open for 0% -> 0% of each run, Pallas kernels for 0% -> 0%
where the time goes in v1:
time: 82.3 us; the launch traced here: 81.2 us
  Pallas kernels  70.3 us (85%)
  local copies, waits for them, and re-layouts  8.6 us (10%)
  between operations  2.33 us (3%)
    pallas_call x1, Pallas kernels, per_device(): pl.pallas_call(functools.partial(kernel, V, VP), out_shape=(jax.ShapeDtyp...  70.3 us
    unnamed x2, local copies, waits for them, and re-layouts  8.6 us

profile of v1, /device:TPU:1, one launch (start us, length us, event | category | flops | bytes accessed | tf_op | source)
XLA Modules:
  0.0 81.2 jit_solution(15321058004343855899)
XLA Ops:
  0.6 7.4 %copy.6.weight = bf16[1024,2376]{1,0:T(8,128)(2,1)} copy(bf16[1024,2376]{0,1:T(8,128)(2,1)} %param.5) | data formatting | bytes 9732096 | tf_op args[1]
  8.1 70.3 %shard_map.59 = (f32[1,48]{1,0:T(1,128)}, f32[1,1]{1,0:T(1,128)}) custom-call(bf16[48,128]{1,0:T(8,128)(2,1)} %hid.1, bf16[1024,2376]{1,0:T(8,128)(2,1)} %copy.6.weight, s32[1,48]{1,0:T(1,128)} %bitcast.4, s32[1,48]{1,0:T(1,128)} %bitcast.5), custom_call_target="tpu_custom_call" | custom-call | tf_op jit(solution)/shard_map/pallas_call | solution.py:312
  78.3 1.2 %copy.9 = f32[48]{0:T(128)} copy(f32[48]{0:T(128)} %bitcast.6) | data formatting | bytes 384

commit v2 on v0

v2 whole, which is shorter than its diff:
```python
import functools

import jax
import jax.numpy as jnp
from jax import lax
from jax.experimental import pallas as pl
from jax.experimental.pallas import tpu as pltpu
from jax.sharding import PartitionSpec as P

NZ, NX, NY, NC = 8, 4, 8, 2
NV = NX * NY * NC
T = 48
D = 128
CH = 16
NCH = T // CH
HALF = 64
LN2 = 0.6931471805599453
TOP = 32766.0
F32 = jnp.float32
scope = jax.named_scope


def kernel(V, VP, hid, weight, tgt, msk, out,
           L, H, W, ACC, SB, RB, TM, ST, MB3,
           in_sem, zs_sem, src_r, own_r, s1_s, s2_s, s2_r,
           q_s, q_r, ring_s, ring_r, st_s, st_r, m_s, m_r, met):
    z = lax.axis_index("dp")
    v = lax.axis_index("vocab")
    c = lax.rem(v, NC)
    y = lax.rem(lax.div(v, NC), NY)
    x = lax.div(v, NC * NY)
    px, py = lax.rem(x, 2), lax.rem(y, 2)
    me = c * 4 + 2 * px + py
    sg = 1 - 2 * c

    def at(dz=0, dx=0, dy=0, dc=0):
        return (lax.rem(z + dz + NZ, NZ),
                (lax.rem(x + dx, NX) * NY + lax.rem(y + dy + NY, NY)) * NC + lax.rem(c + dc, NC))

    def remote(src, dst, ss, rs, dev):
        return pltpu.make_async_remote_copy(
            src_ref=src, dst_ref=dst, send_sem=ss, recv_sem=rs,
            device_id=dev, device_id_type=pl.DeviceIdType.MESH)

    def arrived(ref, sem):
        pltpu.make_async_copy(ref, ref, sem).wait()

    def signal(sem, dev):
        pl.semaphore_signal(sem, inc=1, device_id=dev, device_id_type=pl.DeviceIdType.MESH)

    near = [(dx, dy, dc) for dx, dy in ((1, 1), (3, -1), (1, 0), (3, 0), (0, 1), (0, -1)) for dc in (0, 1)] + [(0, 0, 1)]
    far = [(dx, dy, 0) for dy in (4, 2, -2, 0) for dx in (2, 1, 3, 0)]
    far = [d for d in far if d != (0, 0, 0) and d not in near]
    barrier = pltpu.get_barrier_semaphore()
    with scope("barrier"):
        for dx, dy, dc in far:
            signal(barrier, at(dx=dx, dy=dy, dc=dc))
        for dz in (4, 3, 5, 2, 6, 1, 7):
            signal(barrier, at(dz=dz))
        for dx, dy, dc in near:
            signal(barrier, at(dx=dx, dy=dy, dc=dc))

        wcopy = pltpu.make_async_copy(weight, W, in_sem)
        wcopy.start()
        pl.semaphore_wait(barrier, len(far) + 7 + len(near))

    def rows(o):
        return pl.ds(pl.multiple_of(o * T, CH), T)

    kd = 2 * x + lax.div(y, 4)
    zoff = lax.rem(z - kd + NZ, NZ)
    zmove = remote(hid, L.at[rows(zoff)], zs_sem, src_r.at[zoff], (kd, v))
    zlocal = pltpu.make_async_copy(hid, L.at[rows(0)], src_r.at[0])

    @pl.when(z != kd)
    def _():
        zmove.start()

    @pl.when(z == kd)
    def _():
        zlocal.start()

    tcopy = remote(tgt, TM.at[0], q_s, q_r, at(dz=4))
    mcopy = remote(msk, TM.at[1], q_s, q_r, at(dz=4))
    tcopy.start()
    mcopy.start()
    for dy, dc in ((-1, 0), (-1, 1), (0, 1)):
        signal(met, at(dy=dy, dc=dc))

    is_src = jnp.logical_and(x == lax.div(z, 2), lax.div(y, 4) == lax.rem(z, 2))

    q = lax.rem(y, 4)
    odd = lax.rem(lax.div(q, 2) + x, 2)
    spread = [(dx, dy) for dy in (4, 2, -2, 0) for dx in (2, 0)]
    mine = c * 4 + q

    def s1(o, n):
        dx, dy = spread[n]
        return remote(L.at[rows(o)], H.at[mine, rows(o)], s1_s, own_r.at[o], at(dx=dx + odd, dy=dy))

    def s1_here(o):
        return pltpu.make_async_copy(L.at[rows(o)], H.at[mine, rows(o)], own_r.at[o])

    fx, fy = sg + NX, sg
    hops = [(fx, fy, 1), (fx, fy, 0), (fx, 0, 1), (0, fy, 1), (fx, 0, 0), (0, fy, 0), (0, 0, 1)]

    def s2(o, n):
        b = H.at[me, rows(o)]
        return remote(b, b, s2_s, s2_r.at[o], at(dx=hops[n][0], dy=hops[n][1], dc=hops[n][2]))

    def from_source(*offs):
        with scope(f"src{offs[0]}"):
            @pl.when(is_src)
            def _():
                for o in offs:
                    arrived(L.at[rows(o)], src_r.at[o])
                    for n in range(7):
                        s1(o, n).start()

                    @pl.when(odd == 1)
                    def _():
                        s1(o, 7).start()

                    @pl.when(odd == 0)
                    def _():
                        s1_here(o).start()

    def take_own(*offs):
        with scope(f"own{offs[0]}"):
            for o in offs:
                arrived(H.at[me, rows(o)], own_r.at[o])
                for n in range(len(hops)):
                    s2(o, n).start()

    def take_all(*offs):
        with scope(f"all{offs[0]}"):
            for o in offs:
                arrived(H.at[0, 0:len(hops) * T], s2_r.at[o])

    lane = lax.broadcasted_iota(jnp.int32, (CH, VP), 1)
    valid = lane < V

    def mm(*offs):
        with scope(f"mm{offs[0]}"):
            lhs = jnp.concatenate([
                jnp.concatenate([H[cc * 4 + rr, rows(o), :] for rr in range(4) for cc in range(NC)], axis=1)
                for o in offs], axis=0)
            main = V // 256 * 256
            for a in [*range(0, main, 768), main]:
                w = min(768, main - a) or V - a
                if w:
                    res = lax.dot_general(lhs, W[a:a + w, :], (((1,), (1,)), ((), ())),
                                          preferred_element_type=F32)
                    for n, o in enumerate(offs):
                        ACC[o, :, a:a + w] = res[n * T:(n + 1) * T]

    def part(o, k):
        return ACC[lax.rem(o + NZ, NZ), pl.ds(k * CH, CH), :]

    def taken(n, k):
        q = RB[n, pl.ds(k * CH, CH), :].astype(F32)
        g = jnp.exp(q[:, VP - 1:VP] * (LN2 / 64)) * (1.0 / TOP)
        return q * g

    def ring(n, k):
        b = pl.ds(k * CH, CH)
        return remote(SB.at[n, b], RB.at[n, b], ring_s, ring_r.at[n, k],
                      at(dz=sg if n < 4 else -sg))

    def send(n, k, val):
        top = jnp.max(jnp.where(valid, jnp.abs(val), 0.0), axis=1, keepdims=True)
        code = jnp.ceil(jnp.log(jnp.maximum(top, 1e-30)) * (64 / LN2)) + 1.0
        q = val * (jnp.exp(code * (-LN2 / 64)) * TOP)
        SB[n, pl.ds(k * CH, CH), :] = jnp.round(jnp.where(valid, q, code)).astype(jnp.int16)
        ring(n, k).start()

    def block_of(n):
        return -n * sg if n < 4 else (n - 3) * sg

    def first(n):
        with scope(f"first{n}"):
            for k in range(NCH):
                send(n, k, part(block_of(n), k))

    def onward(n, k):
        with scope(f"ring{n}"):
            ring(n - 1, k).wait_recv()
            send(n, k, part(block_of(n), k) + taken(n - 1, k))

    from_source(0)
    take_own(0)
    from_source(1, 7, 2, 6)
    take_all(0)
    take_own(1, 7)
    take_own(2, 6)
    with scope("wwait"):
        wcopy.wait()
    mm(0)
    first(0)
    from_source(3, 5, 4)
    take_all(1, 7)
    mm(1, 7)
    first(4)
    for k in range(NCH):
        onward(1, k)
    take_own(3, 5, 4)
    take_all(2, 6)
    mm(2, 6)
    for k in range(NCH):
        onward(5, k)
        onward(2, k)
    take_all(3, 5, 4)
    mm(3, 5, 4)
    for k in range(NCH):
        onward(6, k)
        onward(3, k)

    arrived(TM, q_r)
    ri = lax.broadcasted_iota(jnp.int32, (T, T), 0)
    ci = lax.broadcasted_iota(jnp.int32, (T, T), 1)
    tcol = jnp.sum(jnp.where(ri == ci, TM[0].astype(F32), 0.0), axis=1, keepdims=True).astype(jnp.int32)
    ids = jnp.where(valid, lane + v * V, -1)
    lses, picks = [], []
    for k in range(NCH):
        with scope("last"):
            ring(3, k).wait_recv()
            ring(6, k).wait_recv()
        val = part(4, k) + taken(3, k) + taken(6, k)
        val = jnp.where(valid, val, -3e38)
        top = jnp.max(val, axis=1, keepdims=True)
        s = jnp.sum(jnp.exp(val - top), axis=1, keepdims=True)
        picks.append(jnp.sum(jnp.where(ids == tcol[k * CH:(k + 1) * CH], val, 0.0), axis=1, keepdims=True))
        lses.append(top + jnp.log(s))

    rl = lax.broadcasted_iota(jnp.int32, (T, 128), 0)
    ll = lax.broadcasted_iota(jnp.int32, (T, 128), 1)
    both = jnp.where(rl == ll, jnp.concatenate(lses, axis=0),
                     jnp.where(rl + HALF == ll, jnp.concatenate(picks, axis=0), 0.0))
    with scope("plane"):
        pl.semaphore_wait(met, 3)
        ST[v] = jnp.sum(both, axis=0, keepdims=True)

        def stat(d):
            o = lax.rem(v + d, NV)
            return remote(ST.at[v], ST.at[v], st_s, st_r, (z, o))

        for d in range(1, NV):
            stat(d).start()
        arrived(ST.at[0:NV - 1], st_r)
        st = ST[...].reshape(NV, 128)
        top = jnp.max(st, axis=0, keepdims=True)
        lse = top + jnp.log(jnp.sum(jnp.exp(st - top), axis=0, keepdims=True))
        picked = jnp.sum(st, axis=0, keepdims=True)
        nll = TM[1].astype(F32) * (lse[:, :T] - picked[:, HALF:HALF + T])
        total = jnp.sum(nll, axis=1, keepdims=True)

    with scope("zmerge"):
        MB3[z, :, 0:T] = nll
        MB3[z, :, HALF:128] = jnp.broadcast_to(total, (1, 128 - HALF))

        def across(d):
            return remote(MB3.at[z], MB3.at[z], m_s, m_r, at(dz=d))

        for d in (4, 3, 5, 2, 6, 1, 7):
            across(d).start()
        arrived(MB3.at[0:NZ - 1], m_r)
        opp = lax.rem(z + 4, NZ)
        out[:, 0:HALF] = MB3[opp, :, 0:HALF]
        out[:, HALF:128] = sum(MB3[j, :, HALF:128] for j in range(NZ))

    with scope("drain"):
        @pl.when(z != kd)
        def _():
            zmove.wait_send()

        arrived(TM, q_s)

        @pl.when(is_src)
        def _():
            arrived(H.at[0:7], s1_s)

            @pl.when(odd == 1)
            def _():
                arrived(H.at[0], s1_s)

        arrived(H.at[0:len(hops)], s2_s)
        arrived(SB, ring_s)
        arrived(ST.at[0:NV - 1], st_s)
        arrived(MB3.at[0:NZ - 1], m_s)


def per_device(hidden, weight, targets, pad_mask):
    K, V = weight.shape
    VP = -(-(V + 1) // 128) * 128
    hbm = pl.BlockSpec(memory_space=pl.ANY)
    dma = pltpu.SemaphoreType.DMA
    out = pl.pallas_call(
        functools.partial(kernel, V, VP),
        out_shape=jax.ShapeDtypeStruct((1, 128), F32),
        in_specs=[hbm] * 4,
        out_specs=pl.BlockSpec(memory_space=pltpu.VMEM),
        scratch_shapes=[
            pltpu.VMEM((NZ * T, D), jnp.bfloat16),
            pltpu.VMEM((NC * 4, NZ * T, D), jnp.bfloat16),
            pltpu.VMEM((V, K), jnp.bfloat16),
            pltpu.VMEM((8, T, VP), F32),
            pltpu.VMEM((7, T, VP), jnp.int16),
            pltpu.VMEM((7, T, VP), jnp.int16),
            pltpu.VMEM((2, 1, T), jnp.int32),
            pltpu.VMEM((NV, 1, 128), F32),
            pltpu.VMEM((NZ, 1, 128), F32),
            dma, dma, dma((8,)), dma((8,)), dma, dma, dma((8,)),
            dma, dma, dma, dma((7, NCH)), dma, dma, dma, dma,
            pltpu.SemaphoreType.REGULAR,
        ],
        compiler_params=pltpu.CompilerParams(collective_id=0, has_side_effects=True),
    )(hidden, weight.T, targets.reshape(1, T), pad_mask.reshape(1, T))
    return out[0, :T], out[0, HALF]


def solution(mesh):
    placed = (P("dp", "vocab"), P("dp", "vocab"), P("dp"), P("dp"))
    return jax.shard_map(
        per_device, mesh=mesh, in_specs=placed, out_specs=(P("dp"), P()), check_vma=False
    )
```

time: 174 us -> 70.4 us (0.40)
  blocking collectives: 96.9 us -> 0 us
  Pallas kernels: 0 us -> 67 us
  waiting for transfers between devices: 47.3 us -> 0 us
  between operations: 14.2 us -> 0.64 us
  matrix products: 6.42 us -> 0 us
  other arithmetic: 5.12 us -> 0 us
    all_to_all x4 -> x0, blocking collectives: 96.9 us -> none  [the longest x3 64.9 us: from_everyone(): return lax.all_to_all(copies, axis, split_axis=0, concat_axis=0, tiled=True)]
    pallas_call x0 -> x1, Pallas kernels: none -> 67 us  [per_device(): pl.pallas_call(functools.partial(kernel, V, VP), out_shape=jax.ShapeDtype...]
    reduce_scatter x1 -> x0, waiting for transfers between devices: 47.3 us -> none  [per_device(): lax.psum_scatter(jnp.dot(spread, weight, preferred_element_type=jnp.float...]
    dot_general x1 -> x0, matrix products: 6.42 us -> none  [per_device(): jnp.dot(spread, weight, preferred_element_type=jnp.float32)]
    reduce_sum x3 -> x0, other arithmetic: 3.06 us -> none  [the longest x1 1.31 us: per_device(): local_sum = jnp.sum(jnp.exp(logits - local_max[:, None]), axis=1)]
  transfers between devices with their start and end apart: 1 -> 0, of which waited for: 1 -> 0; matrix products, arithmetic and copies ran while one was open for 0% -> 0% of each run, Pallas kernels for 0% -> 0%
where the time goes in v2:
time: 70.4 us; the launch traced here: 70.1 us
  Pallas kernels  67 us (95%)
  local copies, waits for them, and re-layouts  2.45 us (3%)
    pallas_call x1, Pallas kernels, per_device(): pl.pallas_call(functools.partial(kernel, V, VP), out_shape=jax.ShapeDtype...  67 us

profile of v2, /device:TPU:1, one launch (start us, length us, event | category | flops | bytes accessed | tf_op | source)
XLA Modules:
  0.0 70.1 jit_solution(18426766426787130209)
XLA Ops:
  0.6 67.0 %shard_map.59 = f32[1,128]{1,0:T(1,128)} custom-call(bf16[48,128]{1,0:T(8,128)(2,1)} %hid.1, bf16[2376,1024]{1,0:T(8,128)(2,1)} %bitcast.6, s32[1,48]{1,0:T(1,128)} %bitcast.7, s32[1,48]{1,0:T(1,128)} %bitcast.8), custom_call_target="tpu_custom_call" | custom-call | tf_op jit(solution)/shard_map/pallas_call | solution.py:297
  67.6 1.3 %slice.7 = f32[1,1]{1,0:T(1,128)} slice(f32[1,128]{1,0:T(1,128)} %shard_map.59), slice={[0:1], [64:65]} | slice | bytes 8 | tf_op jit(solution)/shard_map/slice | solution.py:318
  68.9 1.2 %slice_bitcast_fusion = f32[48]{0:T(128)} fusion(f32[1,128]{1,0:T(1,128)} %shard_map.59), kind=kLoop, calls=%fused_computation | loop fusion | bytes 384 | tf_op jit(solution)/shard_map/squeeze | solution.py:318
